TPU v7x, 768 devices: a whole 4x8x12 slice. The times are simulated.
768 devices in a mesh: fsdp: 24 (over z, core), grp: 32 (over y, x).
Axes of the slice: x: 4, y: 8, z: 12, core: 2. Of those that a mesh axis runs over, the one named last changes fastest.
Arguments:
- grads: bfloat16 [384, 384, 2048], P('grp', 'fsdp')
- momentum: bfloat16 [384, 384, 2048], P('grp', 'fsdp'), may hold values from -6 to 6
- row_counts: int32 [384], P('grp'), may hold values from 128 to 384, as said below
Outputs:
- update: bfloat16 [384, 384, 2048], P('grp', 'fsdp')
- new_momentum: bfloat16 [384, 384, 2048], P('grp', 'fsdp')
Inputs may be any that keep to these rules, and one draw needn't show every extreme that they name: `row_counts`: each entry is one, two or three times 384 // 3, and some entry equals 384.
All inputs are finite; a program needn't handle non-finite values.
Results may differ from a plain program's by a relative error of at most 0.007.
Values may be sent and summed in bfloat16 or wider, within the bound.
No kernel may reach another device: no remote copies, remote signals or barrier semaphores. Data moves between devices by JAX's collectives and lax.ppermute only.
A program may use at most 32 MiB of HBM per device.

v0:
```python
import functools

import jax
import jax.numpy as jnp
from jax import lax
from jax.sharding import Mesh
from jax.sharding import PartitionSpec as P

ITERS = 2
FSDP = ("fsdp_0", "fsdp_1")
FSDP_GRP = ("fsdp_0", "fsdp_1", "grp_0", "grp_1")
GRP = ("grp_0", "grp_1")


first_coef = 3.4445
second_coef = -4.775
third_coef = 2.0315


def over_axes(x, axes):
    return functools.reduce(lax.psum, axes, x)


def cut_along(x, dim, size):
    dims = x.shape
    pieces = x.reshape(*dims[:dim], size, dims[dim] // size, *dims[dim + 1 :])
    return jnp.moveaxis(pieces, dim, 0)


def laid_out(pieces, dim):
    pieces = jnp.moveaxis(pieces, 0, dim)
    dims = pieces.shape
    return pieces.reshape(*dims[:dim], dims[dim] * dims[dim + 1], *dims[dim + 2 :])


def moved_by_axis(pieces, axes, sequence):
    dims = [lax.axis_size(a) for a in axes]
    pieces = pieces.reshape(*dims, *pieces.shape[1:])
    for k in sequence:
        pieces = lax.all_to_all(pieces, axes[k], split_axis=k, concat_axis=k, tiled=True)
    return pieces.reshape(-1, *pieces.shape[len(axes) :])


def two_step_exchange(x, groups, sequence, split_dim, concat_dim):
    size = lax.axis_size(groups[0]) * lax.axis_size(groups[1])
    pieces = cut_along(x, split_dim, size)
    return laid_out(moved_by_axis(pieces, groups, sequence), concat_dim)


def unchanged(value):
    return value


def orthogonal(matrix, combine):
    frob = jnp.sqrt(combine(jnp.sum(jnp.square(matrix.astype(jnp.float32)))))
    current = (matrix.astype(jnp.float32) / (frob + 1e-07)).astype(jnp.bfloat16)
    for step in range(ITERS):
        partial_gram = jnp.dot(current, current.T, preferred_element_type=jnp.float32)
        gram = combine(partial_gram).astype(jnp.bfloat16)
        square = jnp.dot(gram, gram, preferred_element_type=jnp.float32)
        poly = (second_coef * gram.astype(jnp.float32) + third_coef * square).astype(jnp.bfloat16)
        current = (
            first_coef * current.astype(jnp.float32)
            + jnp.dot(poly, current, preferred_element_type=jnp.float32)
        ).astype(jnp.bfloat16)
    return current


def local(grads, momentum, row_counts):
    matrices, rows_here, width = grads.shape
    offset = lax.axis_index(FSDP) * rows_here
    row_ids = offset + lax.broadcasted_iota(jnp.int32, (1, rows_here, 1), 1)
    live = row_ids < row_counts[:, None, None]
    graded = jnp.where(live, grads.astype(jnp.float32), 0.0)
    live_rows = jnp.sum(jnp.clip(row_counts - offset, 0, rows_here)).astype(jnp.float32)
    square_sum, row_total = (
        over_axes(jnp.sum(graded * graded), FSDP_GRP),
        over_axes(live_rows, FSDP_GRP),
    )
    clip = jnp.minimum(1.0, lax.rsqrt(square_sum / (row_total * width) + 1e-06))
    new_momentum = jnp.where(live, 0.95 * momentum.astype(jnp.float32) + clip * graded, 0.0).astype(
        jnp.bfloat16
    )
    padded = jnp.concatenate([new_momentum, jnp.zeros_like(new_momentum)], axis=0)
    owned = lax.all_to_all(padded, FSDP, split_axis=0, concat_axis=1, tiled=True)
    result = orthogonal(owned[0], unchanged)
    returned = two_step_exchange(result[None], ("fsdp_0", "fsdp_1"), (1, 0), 1, 0)
    final = returned[:matrices]
    update = (0.2 * jnp.sqrt(jnp.float32(width)) * final.astype(jnp.float32)).astype(jnp.bfloat16)
    return (update, new_momentum)


def solution(mesh):
    torus = Mesh(mesh.devices.reshape(12, 2, 8, 4), ("fsdp_0", "fsdp_1", "grp_0", "grp_1"))
    in_specs = (P(GRP, FSDP, None), P(GRP, FSDP, None), P(GRP))
    out_specs = (P(GRP, FSDP, None), P(GRP, FSDP, None))
    return jax.shard_map(local, mesh=torus, in_specs=in_specs, out_specs=out_specs, check_vma=False)
```

profile of v0, /device:TPU:65, one launch (start us, length us, event | category | flops | bytes accessed | tf_op | source)
XLA Modules:
  0.0 213.9 jit_solution(17268714230181078154)
XLA Ops:
  0.7 1.3 clamp_reduce_fusion
  1.9 0.7 broadcast_compare_fusion
  2.7 2.2 %multiply_reduce_fusion = f32[]{:T(128)} fusion(bf16[12,16,2048]{2,1,0:T(8,128)(2,1)} %param.3, pred[12,16]{1,0:T(8,128)(4,1)S(1)} %broadcast_compare_fusion), kind=kLoop, calls=%fused_computation.8 | loop fusion | flops 1572863 | bytes 786628 | tf_op jit(solution)/shard_map/reduce_sum | solution.py:77
  5.5 25.6 %all-reduce.1 = (f32[]{:T(128)}, f32[]{:T(128)}) all-reduce(f32[]{:T(128)} %multiply_reduce_fusion, f32[]{:T(128)S(6)} %convert_element_type.72), channel_id=1, replica_groups=mesh['fsdp_0'=12,'fsdp_1'=2,'grp_0'=8,'grp_1'=4] {'fsdp_0'}, use_global_device_ids=true, to_apply=%region_1.2 | all-reduce | flops 2 | bytes 16 | tf_op jit(solution)/shard_map/psum | solution.py:21
  31.1 8.8 %all-reduce.4 = (f32[]{:T(128)}, f32[]{:T(128)}) all-reduce(f32[]{:T(128)} %get-tuple-element.2, f32[]{:T(128)} %get-tuple-element.3), channel_id=1, replica_groups=mesh['fsdp_0'=12,'fsdp_1'=2,'grp_0'=8,'grp_1'=4] {'fsdp_1'}, use_global_device_ids=true, to_apply=%region_2.3 | all-reduce | flops 2 | bytes 16 | tf_op jit(solution)/shard_map/psum | solution.py:21
  39.9 14.7 %all-reduce.2 = (f32[]{:T(128)}, f32[]{:T(128)}) all-reduce(f32[]{:T(128)} %get-tuple-element.8, f32[]{:T(128)} %get-tuple-element.9), channel_id=1, replica_groups=mesh['fsdp_0'=12,'fsdp_1'=2,'grp_0'=8,'grp_1'=4] {'grp_0'}, use_global_device_ids=true, to_apply=%region_3.4 | all-reduce | flops 2 | bytes 16 | tf_op jit(solution)/shard_map/psum | solution.py:21
  54.6 9.1 %all-reduce.3 = (f32[]{:T(128)}, f32[]{:T(128)}) all-reduce(f32[]{:T(128)} %get-tuple-element.4, f32[]{:T(128)} %get-tuple-element.5), channel_id=1, replica_groups=mesh['fsdp_0'=12,'fsdp_1'=2,'grp_0'=8,'grp_1'=4] {'grp_1'}, use_global_device_ids=true, to_apply=%region_4.5 | all-reduce | flops 2 | bytes 16 | tf_op jit(solution)/shard_map/psum | solution.py:21
  65.0 1.8 select_convert_fusion
  66.9 0.0 copy-start
  66.9 0.2 concatenate.3
  67.0 66.6 %all_to_all.19 = bf16[24,16,2048]{2,1,0:T(8,128)(2,1)S(1)} all-to-all(bf16[24,16,2048]{2,1,0:T(8,128)(2,1)S(1)} %concatenate.3), channel_id=1, replica_groups=mesh['fsdp_0'=12,'fsdp_1'=2,'grp_0'=8,'grp_1'=4] {'fsdp_0','fsdp_1'}, dimensions={0} | all-to-all | bytes 3145728 | tf_op jit(solution)/shard_map/all_to_all | solution.py:85
  133.6 0.0 copy-done
  133.6 1.4 fusion
  135.7 0.4 fusion.1
  136.1 1.0 convolution_convert_fusion.1
  137.1 1.2 add_convert_fusion.1
  138.3 0.0 copy-start.1
  138.3 1.1 copy-done.1
  139.5 1.0 convolution_convert_fusion
  140.5 3.1 %add_convert_fusion = bf16[384,2048]{1,0:T(8,128)(2,1)S(1)} fusion(bf16[384,2048]{1,0:T(8,128)(2,1)} %copy-done.1, bf16[384,384]{1,0:T(8,128)(2,1)S(1)} %convolution_convert_fusion), kind=kOutput, calls=%fused_computation.4 | convolution fusion | flops 721108992 | bytes 3440640 | tf_op jit(solution)/shard_map/dot_general | solution.py:64
  143.6 0.2 copy.5
  143.8 4.6 %all_to_all.20 = bf16[12,2,1,16,2048]{4,3,0,2,1:T(8,128)(2,1)S(1)} all-to-all(bf16[12,2,1,16,2048]{4,3,0,2,1:T(8,128)(2,1)S(1)} %copy.5), channel_id=1, replica_groups=mesh['fsdp_0'=12,'fsdp_1'=2,'grp_0'=8,'grp_1'=4] {'fsdp_1'}, dimensions={1} | all-to-all | bytes 3145728 | tf_op jit(solution)/shard_map/all_to_all | solution.py:40
  148.4 0.2 copy.6
  148.6 64.3 %all_to_all.21 = bf16[12,2,1,16,2048]{4,3,1,2,0:T(8,128)(2,1)S(1)} all-to-all(bf16[12,2,1,16,2048]{4,3,1,2,0:T(8,128)(2,1)S(1)} %copy.6), channel_id=1, replica_groups=mesh['fsdp_0'=12,'fsdp_1'=2,'grp_0'=8,'grp_1'=4] {'fsdp_0'}, dimensions={0} | all-to-all | bytes 3145728 | tf_op jit(solution)/shard_map/all_to_all | solution.py:40
  212.9 1.0 multiply_convert_fusion
  (1 shorter events, 0.0 us)
Async XLA Ops:
  66.9 66.8 %copy-start = (bf16[12,16,2048]{2,1,0:T(8,128)(2,1)}, bf16[12,16,2048]{2,1,0:T(8,128)(2,1)S(1)}, u32[]{:S(2)}) copy-start(bf16[12,16,2048]{2,1,0:T(8,128)(2,1)S(1)} %select_convert_fusion) | copy-start | bytes 2359300
  138.3 1.2 copy-start.1
where the time goes:
time: 214 us
  blocking collectives  194 us (91%)
  other arithmetic  8.88 us (4%)
  matrix products  6.35 us (3%)
  between operations  3.42 us (2%)
    all_to_all x2, blocking collectives, moved_by_axis(): lax.all_to_all(pieces, axes[k], split_axis=k, concat_axis=k, tiled=True)  68.9 us
    all_to_all x1, blocking collectives, local(): lax.all_to_all(padded, FSDP, split_axis=0, concat_axis=1, tiled=True)  66.6 us
    psum x4, blocking collectives, over_axes(): return functools.reduce(lax.psum, axes, x)  58.1 us
    dot_general x2, matrix products, orthogonal(): jnp.dot(poly, current, preferred_element_type=jnp.float32)  4.36 us

commit v1 on v0

v1 whole, which is shorter than its diff:
```python
import jax
import jax.numpy as jnp
from jax import lax
from jax.sharding import Mesh
from jax.sharding import PartitionSpec as P

Z = "fsdp_0"
CORE = "fsdp_1"
FSDP = ("fsdp_0", "fsdp_1")
GRP = ("grp_0", "grp_1")
PLANE = ("fsdp_1", "grp_0", "grp_1")

first_coef = 3.4445
second_coef = -4.775
third_coef = 2.0315


def size_of(axes):
    size = 1
    for axis in axes:
        size *= lax.axis_size(axis)
    return size


def shared_sum(values, axes):
    lanes = lax.broadcasted_iota(jnp.int32, (1, 1, 128), 2)
    row = jnp.zeros((1, 1, 128), jnp.float32)
    for k, value in enumerate(values):
        row = jnp.where(lanes == k, value, row)
    count = size_of(axes)
    rows = lax.all_to_all(
        jnp.broadcast_to(row, (count, 1, 128)), axes, split_axis=0, concat_axis=0, tiled=True
    )
    return [jnp.sum(jnp.where(lanes == k, rows, 0.0)) for k in range(len(values))]


def product(left, right):
    return jnp.dot(left, right, preferred_element_type=jnp.float32)


def polynomials(gram):
    size = gram.shape[0]
    diagonal = lax.broadcasted_iota(jnp.int32, (size, size), 0) == lax.broadcasted_iota(
        jnp.int32, (size, size), 1
    )
    frob = jnp.sqrt(jnp.sum(jnp.where(diagonal, gram, 0.0)))
    inverse = 1.0 / (frob + 1e-07)
    gram0 = (gram * inverse * inverse).astype(jnp.bfloat16)
    poly0 = (
        second_coef * gram0.astype(jnp.float32) + third_coef * product(gram0, gram0)
    ).astype(jnp.bfloat16)
    half = first_coef * gram0.astype(jnp.float32) + product(poly0, gram0)
    gram1 = (first_coef * half + product(half.astype(jnp.bfloat16), poly0)).astype(jnp.bfloat16)
    poly1 = (
        second_coef * gram1.astype(jnp.float32) + third_coef * product(gram1, gram1)
    ).astype(jnp.bfloat16)
    return inverse, poly0, poly1


def applied(poly, x):
    return (first_coef * x.astype(jnp.float32) + product(poly, x)).astype(jnp.bfloat16)


def local(grads, momentum, row_counts):
    matrices, rows_here, width = grads.shape
    offset = lax.axis_index(FSDP) * rows_here
    row_ids = offset + lax.broadcasted_iota(jnp.int32, (1, rows_here, 1), 1)
    live = row_ids < row_counts[:, None, None]
    graded = jnp.where(live, grads.astype(jnp.float32), 0.0)
    (square_sum,) = shared_sum([jnp.sum(graded * graded)], (Z,))
    rows_in_group = jnp.sum(row_counts).astype(jnp.float32)
    square_sum, row_total = shared_sum([square_sum, rows_in_group], PLANE)
    row_total = row_total / lax.axis_size(CORE)
    clip = jnp.minimum(1.0, lax.rsqrt(square_sum / (row_total * width) + 1e-06))
    new_momentum = jnp.where(live, 0.95 * momentum.astype(jnp.float32) + clip * graded, 0.0).astype(
        jnp.bfloat16
    )
    cores = lax.axis_size(CORE)
    half_width = width // cores
    pieces = new_momentum.reshape(matrices, rows_here, cores, half_width).transpose(0, 2, 1, 3)
    pieces = pieces.reshape(matrices * cores, rows_here, half_width)
    owned = lax.all_to_all(pieces, FSDP, split_axis=0, concat_axis=0, tiled=True)
    owned = owned.reshape(-1, half_width)
    part = lax.dot_general(
        owned, owned, (((1,), (1,)), ((), ())), preferred_element_type=jnp.float32
    )
    gram = part + lax.ppermute(part, CORE, [(0, 1), (1, 0)])
    inverse, poly0, poly1 = polynomials(gram)
    x = (owned.astype(jnp.float32) * inverse).astype(jnp.bfloat16)
    x = applied(poly1, applied(poly0, x))
    x = (0.2 * jnp.sqrt(jnp.float32(width)) * x.astype(jnp.float32)).astype(jnp.bfloat16)
    back = lax.all_to_all(
        x.reshape(-1, rows_here, half_width), FSDP, split_axis=0, concat_axis=0, tiled=True
    )
    back = back.reshape(matrices, cores, rows_here, half_width).transpose(0, 2, 1, 3)
    update = back.reshape(matrices, rows_here, width)
    return (update, new_momentum)


def solution(mesh):
    torus = Mesh(mesh.devices.reshape(12, 2, 8, 4), ("fsdp_0", "fsdp_1", "grp_0", "grp_1"))
    in_specs = (P(GRP, FSDP, None), P(GRP, FSDP, None), P(GRP))
    out_specs = (P(GRP, FSDP, None), P(GRP, FSDP, None))
    return jax.shard_map(local, mesh=torus, in_specs=in_specs, out_specs=out_specs, check_vma=False)
```

time: 214 us -> 140 us (0.65)
  the two profiles are of different devices: /device:TPU:65 before, /device:TPU:2 now
where the time goes in v1:
time: 140 us; the launch traced here: 139 us
  blocking collectives  72.4 us (52%)
  starting transfers between devices  27.7 us (20%)
  waiting for transfers between devices  18.9 us (13%)
  other arithmetic  9.15 us (7%)
  local copies, waits for them, and re-layouts  4.4 us (3%)
  between operations  3.54 us (3%)
  matrix products  3.04 us (2%)
    all_to_all x1, blocking collectives, local(): lax.all_to_all(x.reshape(-1, rows_here, half_width), FSDP, split_axis=0,...  36.4 us
    all_to_all x1, blocking collectives, local(): lax.all_to_all(pieces, FSDP, split_axis=0, concat_axis=0, tiled=True)  36 us
    all_to_all x2, starting transfers between devices, shared_sum(): lax.all_to_all(jnp.broadcast_to(row, (count, 1, 128)), axes, split_axis=0...  25.8 us
    all_to_all x2, waiting for transfers between devices, shared_sum(): lax.all_to_all(jnp.broadcast_to(row, (count, 1, 128)), axes, split_axis=0...  16.9 us
  transfers between devices with their start and end apart: 3, of which 3 were waited for; matrix products, arithmetic and copies ran while one was open for 0% of the time, Pallas kernels for 0%

profile of v1, /device:TPU:2, one launch (start us, length us, event | category | flops | bytes accessed | tf_op | source)
XLA Modules:
  0.0 139.2 jit_solution(16656966044999982183)
XLA Ops:
  0.6 0.0 copy-start.2
  0.6 0.0 copy-start.1
  0.7 0.8 broadcast_compare_fusion
  1.5 2.2 %multiply_reduce_fusion = f32[]{:T(128)} fusion(bf16[12,16,2048]{2,1,0:T(8,128)(2,1)} %param.3, pred[12,16]{1,0:T(8,128)(4,1)S(1)} %broadcast_compare_fusion), kind=kLoop, calls=%fused_computation.5 | loop fusion | flops 1572863 | bytes 786628 | tf_op jit(solution)/shard_map/reduce_sum | solution.py:70
  3.7 0.6 broadcast_select_fusion.3
  4.3 0.6 broadcast_in_dim.77
  4.9 15.2 %all-to-all-start = ((f32[12,1,128]{2,1,0:T(1,128)}), f32[12,1,128]{2,1,0:T(1,128)S(1)}, u32[]{:S(2)}, u32[]{:S(2)}) async-start(f32[12,1,128]{2,1,0:T(1,128)} %broadcast_in_dim.77), calls=%async_computation | async-start | bytes 12288 | tf_op jit(solution)/shard_map/all_to_all | solution.py:31
  20.1 0.0 copy-done.2
  20.1 0.6 reduce_sum.54
  21.4 8.7 %all-to-all-done = f32[12,1,128]{2,1,0:T(1,128)S(1)} async-done(((f32[12,1,128]{2,1,0:T(1,128)}), f32[12,1,128]{2,1,0:T(1,128)S(1)}, u32[]{:S(2)}, u32[]{:S(2)}) %all-to-all-start) | async-done | bytes 6176 | tf_op jit(solution)/shard_map/all_to_all | solution.py:31
  30.1 0.6 fusion.11
  30.7 0.6 select_select_fusion
  31.4 0.6 broadcast_in_dim.80
  32.0 10.7 %all-to-all-start.1 = ((f32[64,1,128]{2,1,0:T(1,128)}), f32[64,1,128]{2,1,0:T(1,128)S(1)}, u32[]{:S(2)}, u32[]{:S(2)}) async-start(f32[64,1,128]{2,1,0:T(1,128)} %broadcast_in_dim.80), calls=%async_computation.1 | async-start | bytes 65536 | tf_op jit(solution)/shard_map/all_to_all | solution.py:31
  42.7 8.2 %all-to-all-done.1 = f32[64,1,128]{2,1,0:T(1,128)S(1)} async-done(((f32[64,1,128]{2,1,0:T(1,128)}), f32[64,1,128]{2,1,0:T(1,128)S(1)}, u32[]{:S(2)}, u32[]{:S(2)}) %all-to-all-start.1) | async-done | bytes 32800 | tf_op jit(solution)/shard_map/all_to_all | solution.py:31
  51.0 0.6 reduce_sum.58
  51.6 0.6 reduce_sum.57
  53.5 0.0 copy-done.1
  53.5 1.6 %select_convert_fusion = bf16[12,16,2048]{2,1,0:T(8,128)(2,1)S(1)} fusion(bf16[12,16,2048]{2,1,0:T(8,128)(2,1)S(1)} %copy-done.1, bf16[12,16,2048]{2,1,0:T(8,128)(2,1)} %param.4, f32[]{:T(128)S(6)} %min.3, pred[12,16]{1,0:T(8,128)(4,1)S(1)} %broadcast_compare_fusion), kind=kLoop, calls=%fused_computation.4 | loop fusion | flops 3145728 | bytes 2359492 | tf_op jit(solution)/shard_map/convert_element_type | solution.py:75
  55.1 0.0 copy-start
  55.2 0.1 fusion.14
  55.2 0.8 copy-done
  56.0 0.1 pad_maximum_fusion
  56.1 36.0 %all_to_all.20 = bf16[24,16,1024]{2,1,0:T(8,128)(2,1)S(1)} all-to-all(bf16[24,16,1024]{2,1,0:T(8,128)(2,1)S(1)} %bitcast.19), channel_id=1, replica_groups=mesh['fsdp_0'=12,'fsdp_1'=2,'grp_0'=8,'grp_1'=4] {'fsdp_0','fsdp_1'}, dimensions={0} | all-to-all | bytes 1572864 | tf_op jit(solution)/shard_map/all_to_all | solution.py:82
  92.1 0.6 fusion.15
  92.7 1.9 %collective-permute-start = (f32[384,384]{1,0:T(8,128)S(1)}, f32[384,384]{1,0:T(8,128)S(1)}, u32[]{:S(2)}, u32[]{:S(2)}) collective-permute-start(f32[384,384]{1,0:T(8,128)S(1)} %fusion.15), channel_id=1, source_target_pairs={{0,32},{32,0},{1,33},{33,1},{2,34},{34,2},{3,35},{35,3},{4,36},{36... | collective-permute-start | bytes 1769480 | tf_op jit(solution)/shard_map/ppermute | solution.py:87
  94.7 2.0 %collective-permute-done = f32[384,384]{1,0:T(8,128)S(1)} collective-permute-done((f32[384,384]{1,0:T(8,128)S(1)}, f32[384,384]{1,0:T(8,128)S(1)}, u32[]{:S(2)}, u32[]{:S(2)}) %collective-permute-start) | collective-permute-done | bytes 589856 | tf_op jit(solution)/shard_map/ppermute | solution.py:87
  96.6 0.7 select_reduce_fusion
  98.0 0.4 fusion.2
  98.4 0.3 convolution_add_fusion.1
  98.7 0.6 add_convert_fusion.1
  99.3 0.3 fusion.3
  99.7 0.8 multiply_convert_fusion
  100.5 36.4 %all_to_all.21 = bf16[24,16,1024]{2,1,0:T(8,128)(2,1)S(1)} all-to-all(bf16[24,16,1024]{2,1,0:T(8,128)(2,1)S(1)} %bitcast.22), channel_id=1, replica_groups=mesh['fsdp_0'=12,'fsdp_1'=2,'grp_0'=8,'grp_1'=4] {'fsdp_0','fsdp_1'}, dimensions={0} | all-to-all | bytes 1572864 | tf_op jit(solution)/shard_map/all_to_all | solution.py:92
  136.9 0.8 copy.11
  137.7 1.5 %reshape.90 = bf16[12,16,2048]{2,1,0:T(8,128)(2,1)} reshape(bf16[12,16,2,1024]{3,2,1,0:T(2,128)(2,1)S(1)} %bitcast.21) | data formatting | bytes 1572864 | tf_op jit(solution)/shard_map/reshape | solution.py:96
  (4 shorter events, 0.1 us)
Async XLA Ops:
  0.6 19.5 %copy-start.2 = (s32[12]{0:T(128)S(1)}, s32[12]{0:T(128)}, u32[]{:S(2)}) copy-start(s32[12]{0:T(128)} %param.5) | copy-start | bytes 148
  0.6 52.9 %copy-start.1 = (bf16[12,16,2048]{2,1,0:T(8,128)(2,1)S(1)}, bf16[12,16,2048]{2,1,0:T(8,128)(2,1)}, u32[]{:S(2)}) copy-start(bf16[12,16,2048]{2,1,0:T(8,128)(2,1)} %param.3) | copy-start | bytes 2359300
  4.9 25.2 %all-to-all-start = ((f32[12,1,128]{2,1,0:T(1,128)}), f32[12,1,128]{2,1,0:T(1,128)S(1)}, u32[]{:S(2)}, u32[]{:S(2)}) async-start(f32[12,1,128]{2,1,0:T(1,128)} %broadcast_in_dim.77), calls=%async_computation | async-start | bytes 12288 | tf_op jit(solution)/shard_map/all_to_all | solution.py:31
  32.0 18.9 %all-to-all-start.1 = ((f32[64,1,128]{2,1,0:T(1,128)}), f32[64,1,128]{2,1,0:T(1,128)S(1)}, u32[]{:S(2)}, u32[]{:S(2)}) async-start(f32[64,1,128]{2,1,0:T(1,128)} %broadcast_in_dim.80), calls=%async_computation.1 | async-start | bytes 65536 | tf_op jit(solution)/shard_map/all_to_all | solution.py:31
  55.1 0.9 copy-start
  92.7 3.9 %collective-permute-start = (f32[384,384]{1,0:T(8,128)S(1)}, f32[384,384]{1,0:T(8,128)S(1)}, u32[]{:S(2)}, u32[]{:S(2)}) collective-permute-start(f32[384,384]{1,0:T(8,128)S(1)} %fusion.15), channel_id=1, source_target_pairs={{0,32},{32,0},{1,33},{33,1},{2,34},{34,2},{3,35},{35,3},{4,36},{36... | collective-permute-start | bytes 1769480 | tf_op jit(solution)/shard_map/ppermute | solution.py:87

commit v2 on v1

v2 whole, which is shorter than its diff:
```python
import jax
import jax.numpy as jnp
from jax import lax
from jax.experimental import pallas as pl
from jax.experimental.pallas import tpu as pltpu
from jax.sharding import Mesh
from jax.sharding import PartitionSpec as P

Z = "fsdp_0"
CORE = "fsdp_1"
FSDP = ("fsdp_0", "fsdp_1")
GRP = ("grp_0", "grp_1")
PLANE = ("fsdp_1", "grp_0", "grp_1")
LANES = 128
PARTS = 4
VMEM, SMEM, HBM = pltpu.VMEM, pltpu.SMEM, pltpu.HBM
KERNEL_VMEM = 16 * 1024 * 1024
FIRST_VMEM = 54500000

first_coef = 3.4445
second_coef = -4.775
third_coef = 2.0315


def size_of(axes):
    size = 1
    for axis in axes:
        size *= lax.axis_size(axis)
    return size


def exchanged(pieces, axes):
    return lax.all_to_all(pieces, axes, split_axis=0, concat_axis=0, tiled=True)


def on_core(body, out_shape, places, out_places, scratch=(), limit=KERNEL_VMEM):
    return pl.pallas_call(
        body,
        out_shape=out_shape,
        in_specs=[pl.BlockSpec(memory_space=place) for place in places],
        out_specs=[pl.BlockSpec(memory_space=place) for place in out_places],
        scratch_shapes=scratch,
        compiler_params=pltpu.CompilerParams(vmem_limit_bytes=limit),
    )


def product(left, right):
    return jnp.dot(left, right, preferred_element_type=jnp.float32)


def sum_kernel(
    offset_ref,
    counts_hbm,
    grads_hbm,
    momentum_hbm,
    out_ref,
    grads_ref,
    momentum_ref,
    counts_ref,
    sems,
    counts_sem,
    last_sem,
):
    matrices, rows_here, width = grads_ref.shape
    step = matrices // PARTS
    counted = pltpu.make_async_copy(counts_hbm, counts_ref, counts_sem)
    counted.start()
    copies = [
        pltpu.make_async_copy(
            grads_hbm.at[pl.ds(p * step, step)], grads_ref.at[pl.ds(p * step, step)], sems.at[p]
        )
        for p in range(PARTS)
    ]
    for copy in copies:
        copy.start()
    last = pltpu.make_async_copy(momentum_hbm, momentum_ref, last_sem)
    last.start()
    counted.wait()
    count = jnp.int32(0)
    total = jnp.zeros((rows_here, LANES), jnp.float32)
    for n in range(matrices):
        if n % step == 0:
            copies[n // step].wait()
        part = jnp.zeros((rows_here, LANES), jnp.float32)
        for k in range(width // LANES):
            graded = grads_ref[n, :, k * LANES : (k + 1) * LANES].astype(jnp.float32)
            part = part + graded * graded
        total = total + jnp.where(counts_ref[n] > offset_ref[0], part, 0.0)
        count = count + counts_ref[n]
    row = jnp.sum(total, axis=0, keepdims=True)[None]
    out_ref[:, 0:1, :] = jnp.broadcast_to(row, (out_ref.shape[0], 1, LANES))
    out_ref[:, 1:2, :] = jnp.full((out_ref.shape[0], 1, LANES), count.astype(jnp.float32))
    last.wait()
    for n in range(matrices):

        @pl.when(counts_ref[n] <= offset_ref[0])
        def _():
            grads_ref[n] = jnp.zeros((rows_here, width), jnp.bfloat16)
            momentum_ref[n] = jnp.zeros((rows_here, width), jnp.bfloat16)


def pass_on_kernel(sums_ref, out_ref):
    row = jnp.sum(sums_ref[:, 0:1, :], axis=0, keepdims=True)
    out_ref[:, 0:1, :] = jnp.broadcast_to(row, (out_ref.shape[0], 1, LANES))
    out_ref[:, 1:2, :] = jnp.broadcast_to(sums_ref[0:1, 1:2, :], (out_ref.shape[0], 1, LANES))


def momentum_kernel(cores, sums_ref, grads_ref, momentum_ref, out_ref):
    matrices, _, width = grads_ref.shape
    square_sum = jnp.sum(jnp.sum(sums_ref[:, 0:1, :], axis=0), axis=1, keepdims=True)
    row_total = jnp.sum(sums_ref[:, 1:2, :], axis=0)[:, 0:1] * (1.0 / cores)
    clip = jnp.minimum(1.0, 1.0 / jnp.sqrt(square_sum / (row_total * width) + 1e-06))
    for n in range(matrices):
        mixed = 0.95 * momentum_ref[n].astype(jnp.float32) + clip * grads_ref[n].astype(jnp.float32)
        out_ref[n] = mixed.astype(jnp.bfloat16)


def orthogonal_kernel(scale, mine_ref, other_ref, momentum_ref, out_ref, momentum_hbm, x_ref, sem):
    written = pltpu.make_async_copy(momentum_ref, momentum_hbm, sem)
    written.start()
    here = mine_ref.shape[0]
    size = 2 * here
    x_ref[:here] = mine_ref[...]
    x_ref[here:] = other_ref[...]
    gram = lax.dot_general(
        x_ref[...], x_ref[...], (((1,), (1,)), ((), ())), preferred_element_type=jnp.float32
    )
    diagonal = lax.broadcasted_iota(jnp.int32, (size, size), 0) == lax.broadcasted_iota(
        jnp.int32, (size, size), 1
    )
    frob = jnp.sqrt(
        jnp.sum(
            jnp.sum(jnp.where(diagonal, gram, 0.0), axis=0, keepdims=True), axis=1, keepdims=True
        )
    )
    inverse = 1.0 / (frob + 1e-07)
    gram0 = ((gram * inverse) * inverse).astype(jnp.bfloat16)
    poly0 = (
        second_coef * gram0.astype(jnp.float32) + third_coef * product(gram0, gram0)
    ).astype(jnp.bfloat16)
    half = first_coef * gram0.astype(jnp.float32) + product(poly0, gram0)
    gram1 = (first_coef * half + product(half.astype(jnp.bfloat16), poly0)).astype(jnp.bfloat16)
    poly1 = (
        second_coef * gram1[:here].astype(jnp.float32) + third_coef * product(gram1[:here], gram1)
    ).astype(jnp.bfloat16)
    x_ref[...] = (x_ref[...].astype(jnp.float32) * inverse).astype(jnp.bfloat16)
    x_ref[...] = (
        first_coef * x_ref[...].astype(jnp.float32) + product(poly0, x_ref[...])
    ).astype(jnp.bfloat16)
    x = (
        first_coef * x_ref[:here].astype(jnp.float32) + product(poly1, x_ref[...])
    ).astype(jnp.bfloat16)
    out_ref[...] = (scale * x.astype(jnp.float32)).astype(jnp.bfloat16)
    written.wait()


def local(grads, momentum, row_counts):
    matrices, rows_here, width = grads.shape
    cores = lax.axis_size(CORE)
    offset = (lax.axis_index(FSDP) * rows_here).astype(jnp.int32).reshape(1)
    stack = jax.ShapeDtypeStruct(grads.shape, jnp.bfloat16)
    sums, grads, momentum = on_core(
        sum_kernel,
        [jax.ShapeDtypeStruct((lax.axis_size(Z), 2, LANES), jnp.float32), stack, stack],
        [SMEM, HBM, HBM, HBM],
        [VMEM, VMEM, VMEM],
        [
            pltpu.SMEM((matrices,), jnp.int32),
            pltpu.SemaphoreType.DMA((PARTS,)),
            pltpu.SemaphoreType.DMA,
            pltpu.SemaphoreType.DMA,
        ],
        FIRST_VMEM,
    )(offset, row_counts, grads, momentum)
    sums = exchanged(sums, (Z,))
    (sums,) = on_core(
        pass_on_kernel,
        [jax.ShapeDtypeStruct((size_of(PLANE), 2, LANES), jnp.float32)],
        [VMEM],
        [VMEM],
    )(sums)
    sums = exchanged(sums, PLANE)
    (new_momentum,) = on_core(
        lambda *refs: momentum_kernel(cores, *refs), [stack], [VMEM, VMEM, VMEM], [VMEM]
    )(sums, grads, momentum)
    mine = exchanged(new_momentum, (Z,)).reshape(-1, width)
    other = lax.ppermute(mine, CORE, [(0, 1), (1, 0)])
    scale = 0.2 * width**0.5
    result, new_momentum = on_core(
        lambda *refs: orthogonal_kernel(scale, *refs),
        [jax.ShapeDtypeStruct(mine.shape, jnp.bfloat16), stack],
        [VMEM, VMEM, VMEM],
        [VMEM, HBM],
        [pltpu.VMEM((2 * mine.shape[0], width), jnp.bfloat16), pltpu.SemaphoreType.DMA],
    )(mine, other, new_momentum)
    update = exchanged(result.reshape(grads.shape), (Z,))
    return (update, new_momentum)


def solution(mesh):
    torus = Mesh(mesh.devices.reshape(12, 2, 8, 4), ("fsdp_0", "fsdp_1", "grp_0", "grp_1"))
    in_specs = (P(GRP, FSDP, None), P(GRP, FSDP, None), P(GRP))
    out_specs = (P(GRP, FSDP, None), P(GRP, FSDP, None))
    return jax.shard_map(local, mesh=torus, in_specs=in_specs, out_specs=out_specs, check_vma=False)
```

time: 140 us -> 129 us (0.921)
  the two profiles are of different devices: /device:TPU:2 before, /device:TPU:65 now
where the time goes in v2:
time: 129 us; the launch traced here: 128 us
  blocking collectives  116 us (90%)
  Pallas kernels  5.48 us (4%)
  starting transfers between devices  2.58 us (2%)
  waiting for transfers between devices  1.89 us (1%)
  local copies, waits for them, and re-layouts  1.53 us (1%)
    all_to_all x4, blocking collectives, exchanged(): return lax.all_to_all(pieces, axes, split_axis=0, concat_axis=0, tiled=True)  116 us
    pallas_call x1, Pallas kernels, local(): on_core(lambda *refs: orthogonal_kernel(scale, *refs), [jax.ShapeDtypeStr...  3.46 us
    ppermute x1, starting transfers between devices, local(): other = lax.ppermute(mine, CORE, [(0, 1), (1, 0)])  2.58 us
  transfers between devices with their start and end apart: 1, of which 1 were waited for; matrix products, arithmetic and copies ran while one was open for 0% of the time, Pallas kernels for 0%

profile of v2, /device:TPU:65, one launch (start us, length us, event | category | flops | bytes accessed | tf_op | source)
XLA Modules:
  0.0 128.3 jit_solution(8728958520349343685)
XLA Ops:
  0.6 0.0 copy-start
  0.7 0.6 copy-done
  1.3 1.5 %shard_map.50 = (f32[12,2,128]{2,1,0:T(2,128)S(1)}, bf16[12,16,2048]{2,1,0:T(8,128)(2,1)S(1)}, bf16[12,16,2048]{2,1,0:T(8,128)(2,1)S(1)}) custom-call(s32[1]{0:T(128)} %bitcast.offset_ref, s32[12]{0:T(128)S(1)} %copy-done, bf16[12,16,2048]{2,1,0:T(8,128)(2,1)} %grads_hbm.1, bf16[12,16,2048]{2,1,0:T(8,128)(2,1)} %momentum_hbm.1), custom_call_target="tpu_custom_call" | custom-call | tf_op jit(solution)/shard_map/pallas_call | solution.py:162
  2.8 21.9 %all_to_all.20.sums_ref = f32[12,2,128]{2,1,0:T(2,128)S(1)} all-to-all(f32[12,2,128]{2,1,0:T(2,128)S(1)} %get-tuple-element.7), channel_id=1, replica_groups=mesh['fsdp_0'=12,'fsdp_1'=2,'grp_0'=8,'grp_1'=4] {'fsdp_0'}, dimensions={0} | all-to-all | bytes 24576 | tf_op jit(solution)/shard_map/all_to_all | solution.py:33
  24.8 21.7 %all_to_all.21.refs_0_ = f32[64,2,128]{2,1,0:T(2,128)S(1)} all-to-all(f32[64,2,128]{2,1,0:T(2,128)S(1)} %shard_map.51), channel_id=1, replica_groups=mesh['fsdp_0'=12,'fsdp_1'=2,'grp_0'=8,'grp_1'=4] {'fsdp_1','grp_0','grp_1'}, dimensions={0} | all-to-all | bytes 131072 | tf_op jit(solution)/shard_map/all_to_all | solution.py:33
  46.5 0.4 shard_map.52.refs_2_
  46.9 36.7 %all_to_all.22 = bf16[12,16,2048]{2,1,0:T(8,128)(2,1)S(1)} all-to-all(bf16[12,16,2048]{2,1,0:T(8,128)(2,1)S(1)} %shard_map.52.refs_2_), channel_id=1, replica_groups=mesh['fsdp_0'=12,'fsdp_1'=2,'grp_0'=8,'grp_1'=4] {'fsdp_0'}, dimensions={0} | all-to-all | bytes 1572864 | tf_op jit(solution)/shard_map/all_to_all | solution.py:33
  83.6 2.6 %collective-permute-start = (bf16[192,2048]{1,0:T(8,128)(2,1)S(1)}, bf16[192,2048]{1,0:T(8,128)(2,1)S(1)}, u32[]{:S(2)}, u32[]{:S(2)}) collective-permute-start(bf16[192,2048]{1,0:T(8,128)(2,1)S(1)} %bitcast.3), channel_id=1, source_target_pairs={{0,32},{32,0},{1,33},{33,1},{2,34},{34,2},{3,35},{35,3},{4,36},{36... | collective-permute-start | bytes 2359304 | tf_op jit(solution)/shard_map/ppermute | solution.py:187
  86.2 1.9 %collective-permute-done.refs_1_ = bf16[192,2048]{1,0:T(8,128)(2,1)S(1)} collective-permute-done((bf16[192,2048]{1,0:T(8,128)(2,1)S(1)}, bf16[192,2048]{1,0:T(8,128)(2,1)S(1)}, u32[]{:S(2)}, u32[]{:S(2)}) %collective-permute-start) | collective-permute-done | bytes 786464 | tf_op jit(solution)/shard_map/ppermute | solution.py:187
  88.1 3.5 %shard_map.53 = (bf16[192,2048]{1,0:T(8,128)(2,1)S(1)}, bf16[12,16,2048]{2,1,0:T(8,128)(2,1)}) custom-call(bf16[192,2048]{1,0:T(8,128)(2,1)S(1)} %bitcast.4, bf16[192,2048]{1,0:T(8,128)(2,1)S(1)} %collective-permute-done.refs_1_, bf16[12,16,2048]{2,1,0:T(8,128)(2,1)S(1)} %shard_map.52.refs_2_), custom_call_target="tpu_custom_call" | custom-call | tf_op jit(solution)/shard_map/pallas_call | solution.py:189
  91.6 35.8 %all_to_all.23 = bf16[12,16,2048]{2,1,0:T(8,128)(2,1)S(1)} all-to-all(bf16[12,16,2048]{2,1,0:T(8,128)(2,1)S(1)} %bitcast.5), channel_id=1, replica_groups=mesh['fsdp_0'=12,'fsdp_1'=2,'grp_0'=8,'grp_1'=4] {'fsdp_0'}, dimensions={0} | all-to-all | bytes 1572864 | tf_op jit(solution)/shard_map/all_to_all | solution.py:33
  127.4 0.9 copy.6
  (1 shorter events, 0.0 us)
Async XLA Ops:
  0.6 0.7 copy-start
  83.6 4.5 %collective-permute-start = (bf16[192,2048]{1,0:T(8,128)(2,1)S(1)}, bf16[192,2048]{1,0:T(8,128)(2,1)S(1)}, u32[]{:S(2)}, u32[]{:S(2)}) collective-permute-start(bf16[192,2048]{1,0:T(8,128)(2,1)S(1)} %bitcast.3), channel_id=1, source_target_pairs={{0,32},{32,0},{1,33},{33,1},{2,34},{34,2},{3,35},{35,3},{4,36},{36... | collective-permute-start | bytes 2359304 | tf_op jit(solution)/shard_map/ppermute | solution.py:187

commit v3 on v2

--- a/solution.py
+++ b/solution.py
@@ -10,7 +10,8 @@
 CORE = "fsdp_1"
 FSDP = ("fsdp_0", "fsdp_1")
 GRP = ("grp_0", "grp_1")
-PLANE = ("fsdp_1", "grp_0", "grp_1")
+FIRST = ("fsdp_1", "grp_0", "grp_1")
+SECOND = ("fsdp_0",)
 LANES = 128
 PARTS = 4
 VMEM, SMEM, HBM = pltpu.VMEM, pltpu.SMEM, pltpu.HBM
@@ -100,15 +101,13 @@
 
 
 def pass_on_kernel(sums_ref, out_ref):
-    row = jnp.sum(sums_ref[:, 0:1, :], axis=0, keepdims=True)
-    out_ref[:, 0:1, :] = jnp.broadcast_to(row, (out_ref.shape[0], 1, LANES))
-    out_ref[:, 1:2, :] = jnp.broadcast_to(sums_ref[0:1, 1:2, :], (out_ref.shape[0], 1, LANES))
-
-
-def momentum_kernel(cores, sums_ref, grads_ref, momentum_ref, out_ref):
+    out_ref[...] = jnp.broadcast_to(jnp.sum(sums_ref[...], axis=0, keepdims=True), out_ref.shape)
+
+
+def momentum_kernel(tellers, sums_ref, grads_ref, momentum_ref, out_ref):
     matrices, _, width = grads_ref.shape
     square_sum = jnp.sum(jnp.sum(sums_ref[:, 0:1, :], axis=0), axis=1, keepdims=True)
-    row_total = jnp.sum(sums_ref[:, 1:2, :], axis=0)[:, 0:1] * (1.0 / cores)
+    row_total = jnp.sum(sums_ref[:, 1:2, :], axis=0)[:, 0:1] / tellers
     clip = jnp.minimum(1.0, 1.0 / jnp.sqrt(square_sum / (row_total * width) + 1e-06))
     for n in range(matrices):
         mixed = 0.95 * momentum_ref[n].astype(jnp.float32) + clip * grads_ref[n].astype(jnp.float32)
@@ -156,12 +155,12 @@
 
 def local(grads, momentum, row_counts):
     matrices, rows_here, width = grads.shape
-    cores = lax.axis_size(CORE)
+    tellers = size_of(FSDP)
     offset = (lax.axis_index(FSDP) * rows_here).astype(jnp.int32).reshape(1)
     stack = jax.ShapeDtypeStruct(grads.shape, jnp.bfloat16)
     sums, grads, momentum = on_core(
         sum_kernel,
-        [jax.ShapeDtypeStruct((lax.axis_size(Z), 2, LANES), jnp.float32), stack, stack],
+        [jax.ShapeDtypeStruct((size_of(FIRST), 2, LANES), jnp.float32), stack, stack],
         [SMEM, HBM, HBM, HBM],
         [VMEM, VMEM, VMEM],
         [
@@ -172,16 +171,16 @@
         ],
         FIRST_VMEM,
     )(offset, row_counts, grads, momentum)
-    sums = exchanged(sums, (Z,))
+    sums = exchanged(sums, FIRST)
     (sums,) = on_core(
         pass_on_kernel,
-        [jax.ShapeDtypeStruct((size_of(PLANE), 2, LANES), jnp.float32)],
+        [jax.ShapeDtypeStruct((size_of(SECOND), 2, LANES), jnp.float32)],
         [VMEM],
         [VMEM],
     )(sums)
-    sums = exchanged(sums, PLANE)
+    sums = exchanged(sums, SECOND)
     (new_momentum,) = on_core(
-        lambda *refs: momentum_kernel(cores, *refs), [stack], [VMEM, VMEM, VMEM], [VMEM]
+        lambda *refs: momentum_kernel(tellers, *refs), [stack], [VMEM, VMEM, VMEM], [VMEM]
     )(sums, grads, momentum)
     mine = exchanged(new_momentum, (Z,)).reshape(-1, width)
     other = lax.ppermute(mine, CORE, [(0, 1), (1, 0)])

time: 129 us -> 127 us (0.984)
    all_to_all x4, blocking collectives: 116 us -> 115 us  [exchanged(): return lax.all_to_all(pieces, axes, split_axis=0, concat_axis=0, tiled=True)]
where the time goes in v3:
time: 127 us
  blocking collectives  115 us (91%)
  Pallas kernels  5.48 us (4%)
  starting transfers between devices  2.51 us (2%)
  waiting for transfers between devices  1.89 us (1%)
  local copies, waits for them, and re-layouts  1.53 us (1%)
    all_to_all x4, blocking collectives, exchanged(): return lax.all_to_all(pieces, axes, split_axis=0, concat_axis=0, tiled=True)  115 us
    pallas_call x1, Pallas kernels, local(): on_core(lambda *refs: orthogonal_kernel(scale, *refs), [jax.ShapeDtypeStr...  3.48 us
  transfers between devices with their start and end apart: 1, of which 1 were waited for; matrix products, arithmetic and copies ran while one was open for 0% of the time, Pallas kernels for 0%

profile of v3, /device:TPU:65, one launch (start us, length us, event | category | flops | bytes accessed | tf_op | source)
XLA Modules:
  0.0 126.7 jit_solution(9750816155041351016)
XLA Ops:
  0.6 0.0 copy-start
  0.7 0.6 copy-done
  1.3 1.5 %shard_map.50 = (f32[64,2,128]{2,1,0:T(2,128)S(1)}, bf16[12,16,2048]{2,1,0:T(8,128)(2,1)S(1)}, bf16[12,16,2048]{2,1,0:T(8,128)(2,1)S(1)}) custom-call(s32[1]{0:T(128)} %bitcast.offset_ref, s32[12]{0:T(128)S(1)} %copy-done, bf16[12,16,2048]{2,1,0:T(8,128)(2,1)} %grads_hbm.1, bf16[12,16,2048]{2,1,0:T(8,128)(2,1)} %momentum_hbm.1), custom_call_target="tpu_custom_call" | custom-call | tf_op jit(solution)/shard_map/pallas_call | solution.py:161
  2.8 20.3 %all_to_all.20.sums_ref = f32[64,2,128]{2,1,0:T(2,128)S(1)} all-to-all(f32[64,2,128]{2,1,0:T(2,128)S(1)} %get-tuple-element.7), channel_id=1, replica_groups=mesh['fsdp_0'=12,'fsdp_1'=2,'grp_0'=8,'grp_1'=4] {'fsdp_1','grp_0','grp_1'}, dimensions={0} | all-to-all | bytes 131072 | tf_op jit(solution)/shard_map/all_to_all | solution.py:34
  23.1 0.1 shard_map.51
  23.2 21.9 %all_to_all.21.refs_0_ = f32[12,2,128]{2,1,0:T(2,128)S(1)} all-to-all(f32[12,2,128]{2,1,0:T(2,128)S(1)} %shard_map.51), channel_id=1, replica_groups=mesh['fsdp_0'=12,'fsdp_1'=2,'grp_0'=8,'grp_1'=4] {'fsdp_0'}, dimensions={0} | all-to-all | bytes 24576 | tf_op jit(solution)/shard_map/all_to_all | solution.py:34
  45.1 0.4 shard_map.52.refs_2_
  45.5 36.8 %all_to_all.22 = bf16[12,16,2048]{2,1,0:T(8,128)(2,1)S(1)} all-to-all(bf16[12,16,2048]{2,1,0:T(8,128)(2,1)S(1)} %shard_map.52.refs_2_), channel_id=1, replica_groups=mesh['fsdp_0'=12,'fsdp_1'=2,'grp_0'=8,'grp_1'=4] {'fsdp_0'}, dimensions={0} | all-to-all | bytes 1572864 | tf_op jit(solution)/shard_map/all_to_all | solution.py:34
  82.3 2.5 %collective-permute-start = (bf16[192,2048]{1,0:T(8,128)(2,1)S(1)}, bf16[192,2048]{1,0:T(8,128)(2,1)S(1)}, u32[]{:S(2)}, u32[]{:S(2)}) collective-permute-start(bf16[192,2048]{1,0:T(8,128)(2,1)S(1)} %bitcast.3), channel_id=1, source_target_pairs={{0,32},{32,0},{1,33},{33,1},{2,34},{34,2},{3,35},{35,3},{4,36},{36... | collective-permute-start | bytes 2359304 | tf_op jit(solution)/shard_map/ppermute | solution.py:186
  84.8 1.9 %collective-permute-done.refs_1_ = bf16[192,2048]{1,0:T(8,128)(2,1)S(1)} collective-permute-done((bf16[192,2048]{1,0:T(8,128)(2,1)S(1)}, bf16[192,2048]{1,0:T(8,128)(2,1)S(1)}, u32[]{:S(2)}, u32[]{:S(2)}) %collective-permute-start) | collective-permute-done | bytes 786464 | tf_op jit(solution)/shard_map/ppermute | solution.py:186
  86.7 3.5 %shard_map.53 = (bf16[192,2048]{1,0:T(8,128)(2,1)S(1)}, bf16[12,16,2048]{2,1,0:T(8,128)(2,1)}) custom-call(bf16[192,2048]{1,0:T(8,128)(2,1)S(1)} %bitcast.4, bf16[192,2048]{1,0:T(8,128)(2,1)S(1)} %collective-permute-done.refs_1_, bf16[12,16,2048]{2,1,0:T(8,128)(2,1)S(1)} %shard_map.52.refs_2_), custom_call_target="tpu_custom_call" | custom-call | tf_op jit(solution)/shard_map/pallas_call | solution.py:188
  90.2 35.7 %all_to_all.23 = bf16[12,16,2048]{2,1,0:T(8,128)(2,1)S(1)} all-to-all(bf16[12,16,2048]{2,1,0:T(8,128)(2,1)S(1)} %bitcast.5), channel_id=1, replica_groups=mesh['fsdp_0'=12,'fsdp_1'=2,'grp_0'=8,'grp_1'=4] {'fsdp_0'}, dimensions={0} | all-to-all | bytes 1572864 | tf_op jit(solution)/shard_map/all_to_all | solution.py:34
  125.8 0.9 copy.6
Async XLA Ops:
  0.6 0.7 copy-start
  82.3 4.4 %collective-permute-start = (bf16[192,2048]{1,0:T(8,128)(2,1)S(1)}, bf16[192,2048]{1,0:T(8,128)(2,1)S(1)}, u32[]{:S(2)}, u32[]{:S(2)}) collective-permute-start(bf16[192,2048]{1,0:T(8,128)(2,1)S(1)} %bitcast.3), channel_id=1, source_target_pairs={{0,32},{32,0},{1,33},{33,1},{2,34},{34,2},{3,35},{35,3},{4,36},{36... | collective-permute-start | bytes 2359304 | tf_op jit(solution)/shard_map/ppermute | solution.py:186

commit v4 on v3

--- a/solution.py
+++ b/solution.py
@@ -114,16 +114,39 @@
         out_ref[n] = mixed.astype(jnp.bfloat16)
 
 
-def orthogonal_kernel(scale, mine_ref, other_ref, momentum_ref, out_ref, momentum_hbm, x_ref, sem):
+def product_by_rows(left, right):
+    return lax.dot_general(
+        left, right, (((1,), (1,)), ((), ())), preferred_element_type=jnp.float32
+    )
+
+
+def own_gram_kernel(mine_ref, gram_ref):
+    gram_ref[...] = product_by_rows(mine_ref[...], mine_ref[...])
+
+
+def orthogonal_kernel(
+    scale,
+    mine_ref,
+    other_ref,
+    own_ref,
+    momentum_ref,
+    out_ref,
+    momentum_hbm,
+    x_ref,
+    gram_ref,
+    sem,
+):
     written = pltpu.make_async_copy(momentum_ref, momentum_hbm, sem)
     written.start()
     here = mine_ref.shape[0]
     size = 2 * here
     x_ref[:here] = mine_ref[...]
     x_ref[here:] = other_ref[...]
-    gram = lax.dot_general(
-        x_ref[...], x_ref[...], (((1,), (1,)), ((), ())), preferred_element_type=jnp.float32
-    )
+    rest = product_by_rows(other_ref[...], x_ref[...])
+    gram_ref[:here, :here] = own_ref[...]
+    gram_ref[here:] = rest
+    gram_ref[:here, here:] = rest[:, :here].T
+    gram = gram_ref[...]
     diagonal = lax.broadcasted_iota(jnp.int32, (size, size), 0) == lax.broadcasted_iota(
         jnp.int32, (size, size), 1
     )
@@ -184,14 +207,22 @@
     )(sums, grads, momentum)
     mine = exchanged(new_momentum, (Z,)).reshape(-1, width)
     other = lax.ppermute(mine, CORE, [(0, 1), (1, 0)])
+    here = mine.shape[0]
+    (own,) = on_core(
+        own_gram_kernel, [jax.ShapeDtypeStruct((here, here), jnp.float32)], [VMEM], [VMEM]
+    )(mine)
     scale = 0.2 * width**0.5
     result, new_momentum = on_core(
         lambda *refs: orthogonal_kernel(scale, *refs),
         [jax.ShapeDtypeStruct(mine.shape, jnp.bfloat16), stack],
-        [VMEM, VMEM, VMEM],
+        [VMEM, VMEM, VMEM, VMEM],
         [VMEM, HBM],
-        [pltpu.VMEM((2 * mine.shape[0], width), jnp.bfloat16), pltpu.SemaphoreType.DMA],
-    )(mine, other, new_momentum)
+        [
+            pltpu.VMEM((2 * here, width), jnp.bfloat16),
+            pltpu.VMEM((2 * here, 2 * here), jnp.float32),
+            pltpu.SemaphoreType.DMA,
+        ],
+    )(mine, other, own, new_momentum)
     update = exchanged(result.reshape(grads.shape), (Z,))
     return (update, new_momentum)
 

time: 127 us -> 127 us (level)
  no operation moved by 1% of the time
where the time goes in v4:
time: 127 us; the launch traced here: 126 us
  blocking collectives  115 us (91%)
  Pallas kernels  5.64 us (4%)
  starting transfers between devices  2.51 us (2%)
  local copies, waits for them, and re-layouts  1.53 us (1%)
  waiting for transfers between devices  1.5 us (1%)
    all_to_all x4, blocking collectives, exchanged(): return lax.all_to_all(pieces, axes, split_axis=0, concat_axis=0, tiled=True)  115 us
    pallas_call x1, Pallas kernels, local(): on_core(lambda *refs: orthogonal_kernel(scale, *refs), [jax.ShapeDtypeStr...  3.26 us
  transfers between devices with their start and end apart: 1, of which 1 were waited for; matrix products, arithmetic and copies ran while one was open for 0% of the time, Pallas kernels for 0%

profile of v4, /device:TPU:65, one launch (start us, length us, event | category | flops | bytes accessed | tf_op | source)
XLA Modules:
  0.0 126.5 jit_solution(9316243009918186896)
XLA Ops:
  0.6 0.0 copy-start
  0.7 0.6 copy-done
  1.3 1.5 %shard_map.50 = (f32[64,2,128]{2,1,0:T(2,128)S(1)}, bf16[12,16,2048]{2,1,0:T(8,128)(2,1)S(1)}, bf16[12,16,2048]{2,1,0:T(8,128)(2,1)S(1)}) custom-call(s32[1]{0:T(128)} %bitcast.offset_ref, s32[12]{0:T(128)S(1)} %copy-done, bf16[12,16,2048]{2,1,0:T(8,128)(2,1)} %grads_hbm.1, bf16[12,16,2048]{2,1,0:T(8,128)(2,1)} %momentum_hbm.1), custom_call_target="tpu_custom_call" | custom-call | tf_op jit(solution)/shard_map/pallas_call | solution.py:184
  2.8 20.3 %all_to_all.20.sums_ref = f32[64,2,128]{2,1,0:T(2,128)S(1)} all-to-all(f32[64,2,128]{2,1,0:T(2,128)S(1)} %get-tuple-element.7), channel_id=1, replica_groups=mesh['fsdp_0'=12,'fsdp_1'=2,'grp_0'=8,'grp_1'=4] {'fsdp_1','grp_0','grp_1'}, dimensions={0} | all-to-all | bytes 131072 | tf_op jit(solution)/shard_map/all_to_all | solution.py:34
  23.1 0.1 shard_map.51
  23.2 21.9 %all_to_all.21.refs_0_ = f32[12,2,128]{2,1,0:T(2,128)S(1)} all-to-all(f32[12,2,128]{2,1,0:T(2,128)S(1)} %shard_map.51), channel_id=1, replica_groups=mesh['fsdp_0'=12,'fsdp_1'=2,'grp_0'=8,'grp_1'=4] {'fsdp_0'}, dimensions={0} | all-to-all | bytes 24576 | tf_op jit(solution)/shard_map/all_to_all | solution.py:34
  45.1 0.4 shard_map.52.refs_3_
  45.5 36.8 %all_to_all.22 = bf16[12,16,2048]{2,1,0:T(8,128)(2,1)S(1)} all-to-all(bf16[12,16,2048]{2,1,0:T(8,128)(2,1)S(1)} %shard_map.52.refs_3_), channel_id=1, replica_groups=mesh['fsdp_0'=12,'fsdp_1'=2,'grp_0'=8,'grp_1'=4] {'fsdp_0'}, dimensions={0} | all-to-all | bytes 1572864 | tf_op jit(solution)/shard_map/all_to_all | solution.py:34
  82.3 2.5 %collective-permute-start = (bf16[192,2048]{1,0:T(8,128)(2,1)S(1)}, bf16[192,2048]{1,0:T(8,128)(2,1)S(1)}, u32[]{:S(2)}, u32[]{:S(2)}) collective-permute-start(bf16[192,2048]{1,0:T(8,128)(2,1)S(1)} %bitcast.3), channel_id=1, source_target_pairs={{0,32},{32,0},{1,33},{33,1},{2,34},{34,2},{3,35},{35,3},{4,36},{36... | collective-permute-start | bytes 2359304 | tf_op jit(solution)/shard_map/ppermute | solution.py:209
  84.8 0.4 shard_map.53.refs_2_
  85.2 1.5 %collective-permute-done.refs_1_ = bf16[192,2048]{1,0:T(8,128)(2,1)S(1)} collective-permute-done((bf16[192,2048]{1,0:T(8,128)(2,1)S(1)}, bf16[192,2048]{1,0:T(8,128)(2,1)S(1)}, u32[]{:S(2)}, u32[]{:S(2)}) %collective-permute-start) | collective-permute-done | bytes 786464 | tf_op jit(solution)/shard_map/ppermute | solution.py:209
  86.7 3.3 %shard_map.54 = (bf16[192,2048]{1,0:T(8,128)(2,1)S(1)}, bf16[12,16,2048]{2,1,0:T(8,128)(2,1)}) custom-call(bf16[192,2048]{1,0:T(8,128)(2,1)S(1)} %bitcast.5, bf16[192,2048]{1,0:T(8,128)(2,1)S(1)} %collective-permute-done.refs_1_, f32[192,192]{1,0:T(8,128)S(1)} %shard_map.53.refs_2_, bf16[12,16,2048]{2,1,0:T(8,128)(2,1)S(1)} %shard_map.52.refs_3_), custom_call_target="tpu_custom_call" | custom-call | tf_op jit(solution)/shard_map/pallas_call | solution.py:215
  90.0 35.7 %all_to_all.23 = bf16[12,16,2048]{2,1,0:T(8,128)(2,1)S(1)} all-to-all(bf16[12,16,2048]{2,1,0:T(8,128)(2,1)S(1)} %bitcast.6), channel_id=1, replica_groups=mesh['fsdp_0'=12,'fsdp_1'=2,'grp_0'=8,'grp_1'=4] {'fsdp_0'}, dimensions={0} | all-to-all | bytes 1572864 | tf_op jit(solution)/shard_map/all_to_all | solution.py:34
  125.6 0.9 copy.6
Async XLA Ops:
  0.6 0.7 copy-start
  82.3 4.4 %collective-permute-start = (bf16[192,2048]{1,0:T(8,128)(2,1)S(1)}, bf16[192,2048]{1,0:T(8,128)(2,1)S(1)}, u32[]{:S(2)}, u32[]{:S(2)}) collective-permute-start(bf16[192,2048]{1,0:T(8,128)(2,1)S(1)} %bitcast.3), channel_id=1, source_target_pairs={{0,32},{32,0},{1,33},{33,1},{2,34},{34,2},{3,35},{35,3},{4,36},{36... | collective-permute-start | bytes 2359304 | tf_op jit(solution)/shard_map/ppermute | solution.py:209

commit v5 on v4

--- a/solution.py
+++ b/solution.py
@@ -140,12 +140,11 @@
     written.start()
     here = mine_ref.shape[0]
     size = 2 * here
-    x_ref[:here] = mine_ref[...]
-    x_ref[here:] = other_ref[...]
-    rest = product_by_rows(other_ref[...], x_ref[...])
+    mixed = product_by_rows(other_ref[...], mine_ref[...])
     gram_ref[:here, :here] = own_ref[...]
-    gram_ref[here:] = rest
-    gram_ref[:here, here:] = rest[:, :here].T
+    gram_ref[here:, :here] = mixed
+    gram_ref[:here, here:] = mixed.T
+    gram_ref[here:, here:] = product_by_rows(other_ref[...], other_ref[...])
     gram = gram_ref[...]
     diagonal = lax.broadcasted_iota(jnp.int32, (size, size), 0) == lax.broadcasted_iota(
         jnp.int32, (size, size), 1
@@ -165,7 +164,8 @@
     poly1 = (
         second_coef * gram1[:here].astype(jnp.float32) + third_coef * product(gram1[:here], gram1)
     ).astype(jnp.bfloat16)
-    x_ref[...] = (x_ref[...].astype(jnp.float32) * inverse).astype(jnp.bfloat16)
+    x_ref[:here] = (mine_ref[...].astype(jnp.float32) * inverse).astype(jnp.bfloat16)
+    x_ref[here:] = (other_ref[...].astype(jnp.float32) * inverse).astype(jnp.bfloat16)
     x_ref[...] = (
         first_coef * x_ref[...].astype(jnp.float32) + product(poly0, x_ref[...])
     ).astype(jnp.bfloat16)

time: 127 us -> 127 us (level)
  no operation moved by 1% of the time
where the time goes in v5:
time: 127 us; the launch traced here: 126 us
  blocking collectives  115 us (91%)
  Pallas kernels  5.59 us (4%)
  starting transfers between devices  2.51 us (2%)
  local copies, waits for them, and re-layouts  1.53 us (1%)
  waiting for transfers between devices  1.5 us (1%)
    all_to_all x4, blocking collectives, exchanged(): return lax.all_to_all(pieces, axes, split_axis=0, concat_axis=0, tiled=True)  115 us
    pallas_call x1, Pallas kernels, local(): on_core(lambda *refs: orthogonal_kernel(scale, *refs), [jax.ShapeDtypeStr...  3.21 us
  transfers between devices with their start and end apart: 1, of which 1 were waited for; matrix products, arithmetic and copies ran while one was open for 0% of the time, Pallas kernels for 0%

profile of v5, /device:TPU:65, one launch (start us, length us, event | category | flops | bytes accessed | tf_op | source)
XLA Modules:
  0.0 126.4 jit_solution(17482859125396349626)
XLA Ops:
  0.6 0.0 copy-start
  0.7 0.6 copy-done
  1.3 1.5 %shard_map.50 = (f32[64,2,128]{2,1,0:T(2,128)S(1)}, bf16[12,16,2048]{2,1,0:T(8,128)(2,1)S(1)}, bf16[12,16,2048]{2,1,0:T(8,128)(2,1)S(1)}) custom-call(s32[1]{0:T(128)} %bitcast.offset_ref, s32[12]{0:T(128)S(1)} %copy-done, bf16[12,16,2048]{2,1,0:T(8,128)(2,1)} %grads_hbm.1, bf16[12,16,2048]{2,1,0:T(8,128)(2,1)} %momentum_hbm.1), custom_call_target="tpu_custom_call" | custom-call | tf_op jit(solution)/shard_map/pallas_call | solution.py:184
  2.8 20.3 %all_to_all.20.sums_ref = f32[64,2,128]{2,1,0:T(2,128)S(1)} all-to-all(f32[64,2,128]{2,1,0:T(2,128)S(1)} %get-tuple-element.7), channel_id=1, replica_groups=mesh['fsdp_0'=12,'fsdp_1'=2,'grp_0'=8,'grp_1'=4] {'fsdp_1','grp_0','grp_1'}, dimensions={0} | all-to-all | bytes 131072 | tf_op jit(solution)/shard_map/all_to_all | solution.py:34
  23.1 0.1 shard_map.51
  23.2 21.9 %all_to_all.21.refs_0_ = f32[12,2,128]{2,1,0:T(2,128)S(1)} all-to-all(f32[12,2,128]{2,1,0:T(2,128)S(1)} %shard_map.51), channel_id=1, replica_groups=mesh['fsdp_0'=12,'fsdp_1'=2,'grp_0'=8,'grp_1'=4] {'fsdp_0'}, dimensions={0} | all-to-all | bytes 24576 | tf_op jit(solution)/shard_map/all_to_all | solution.py:34
  45.1 0.4 shard_map.52.refs_3_
  45.5 36.8 %all_to_all.22 = bf16[12,16,2048]{2,1,0:T(8,128)(2,1)S(1)} all-to-all(bf16[12,16,2048]{2,1,0:T(8,128)(2,1)S(1)} %shard_map.52.refs_3_), channel_id=1, replica_groups=mesh['fsdp_0'=12,'fsdp_1'=2,'grp_0'=8,'grp_1'=4] {'fsdp_0'}, dimensions={0} | all-to-all | bytes 1572864 | tf_op jit(solution)/shard_map/all_to_all | solution.py:34
  82.3 2.5 %collective-permute-start = (bf16[192,2048]{1,0:T(8,128)(2,1)S(1)}, bf16[192,2048]{1,0:T(8,128)(2,1)S(1)}, u32[]{:S(2)}, u32[]{:S(2)}) collective-permute-start(bf16[192,2048]{1,0:T(8,128)(2,1)S(1)} %bitcast.3), channel_id=1, source_target_pairs={{0,32},{32,0},{1,33},{33,1},{2,34},{34,2},{3,35},{35,3},{4,36},{36... | collective-permute-start | bytes 2359304 | tf_op jit(solution)/shard_map/ppermute | solution.py:209
  84.8 0.4 shard_map.53.refs_2_
  85.2 1.5 %collective-permute-done.refs_1_ = bf16[192,2048]{1,0:T(8,128)(2,1)S(1)} collective-permute-done((bf16[192,2048]{1,0:T(8,128)(2,1)S(1)}, bf16[192,2048]{1,0:T(8,128)(2,1)S(1)}, u32[]{:S(2)}, u32[]{:S(2)}) %collective-permute-start) | collective-permute-done | bytes 786464 | tf_op jit(solution)/shard_map/ppermute | solution.py:209
  86.7 3.2 %shard_map.54 = (bf16[192,2048]{1,0:T(8,128)(2,1)S(1)}, bf16[12,16,2048]{2,1,0:T(8,128)(2,1)}) custom-call(bf16[192,2048]{1,0:T(8,128)(2,1)S(1)} %bitcast.5, bf16[192,2048]{1,0:T(8,128)(2,1)S(1)} %collective-permute-done.refs_1_, f32[192,192]{1,0:T(8,128)S(1)} %shard_map.53.refs_2_, bf16[12,16,2048]{2,1,0:T(8,128)(2,1)S(1)} %shard_map.52.refs_3_), custom_call_target="tpu_custom_call" | custom-call | tf_op jit(solution)/shard_map/pallas_call | solution.py:215
  89.9 35.7 %all_to_all.23 = bf16[12,16,2048]{2,1,0:T(8,128)(2,1)S(1)} all-to-all(bf16[12,16,2048]{2,1,0:T(8,128)(2,1)S(1)} %bitcast.6), channel_id=1, replica_groups=mesh['fsdp_0'=12,'fsdp_1'=2,'grp_0'=8,'grp_1'=4] {'fsdp_0'}, dimensions={0} | all-to-all | bytes 1572864 | tf_op jit(solution)/shard_map/all_to_all | solution.py:34
  125.6 0.9 copy.6
Async XLA Ops:
  0.6 0.7 copy-start
  82.3 4.4 %collective-permute-start = (bf16[192,2048]{1,0:T(8,128)(2,1)S(1)}, bf16[192,2048]{1,0:T(8,128)(2,1)S(1)}, u32[]{:S(2)}, u32[]{:S(2)}) collective-permute-start(bf16[192,2048]{1,0:T(8,128)(2,1)S(1)} %bitcast.3), channel_id=1, source_target_pairs={{0,32},{32,0},{1,33},{33,1},{2,34},{34,2},{3,35},{35,3},{4,36},{36... | collective-permute-start | bytes 2359304 | tf_op jit(solution)/shard_map/ppermute | solution.py:209
